TPU v7x, 32 devices: a whole 2x2x4 slice. The times are simulated.
32 devices in a mesh: blk: 8 (over z, y), layer: 4 (over x, core).
Axes of the slice: x: 2, y: 2, z: 4, core: 2. Of those that a mesh axis runs over, the one named last changes fastest.
Arguments:
- leaf_area: float32 [12, 16, 1024], P(None, 'layer', 'blk'), may hold values from 0 to 6
- soil_water: float32 [10, 1024], P(None, 'blk'), may hold values from 0.05 to 0.5
- root_share: float32 [16, 10], P('layer'), may hold values from 0 to 0.3
- patch_weight: float32 [16, 32768], P('layer', 'blk'), may hold values from 0 to 1
- patch_owner: int32 [32768, 1], P('blk'), may hold values from 0 to 7; in each aligned block of 4096 rows (0 to 4095, 4096 to 8191, ...) at most 1024 rows name the same one
- patch_local: int32 [32768], P('blk'), may hold values from 0 to 127
- month: int32 [1], replicated, may hold values from 0 to 11
- mix: float32 [1], replicated, may hold values from 0.1 to 0.9
Outputs:
- canopy_share: float32 [16, 1024], P('layer', 'blk')
Inputs may be any that keep to these rules, and one draw needn't show every extreme that they name: `patch_owner`: among the rows of one device, no owner is named more than 1024 times, a bound that some block reaches.
All inputs are finite; a program needn't handle non-finite values.
Results may differ from a plain program's by a relative error of at most 0.000065.
Values sent between devices are 32-bit elements; how exact they have to be, the bound alone decides.
A program may use at most 64 MiB of HBM per device.

v0:
```python
import jax
import jax.numpy as jnp
from jax import lax
from jax.sharding import PartitionSpec as P


def interpolate(leaf_area, month, mix):
    earlier_index = month[0]
    second = (earlier_index + 1) % leaf_area.shape[0]
    earlier = lax.dynamic_index_in_dim(leaf_area, earlier_index, 0, keepdims=False)
    later = lax.dynamic_index_in_dim(leaf_area, second, 0, keepdims=False)
    return mix[0] * earlier + (1.0 - mix[0]) * later


def canopy_terms(patch_weight, patch_leaf, patch_soil, root_share):
    stress = jnp.dot(root_share, patch_soil, precision=lax.Precision.HIGHEST)
    return patch_weight * (1.0 - jnp.exp(-0.5 * patch_leaf)) * stress


def exact_dot(left, right):
    return jnp.dot(left, right, precision=lax.Precision.HIGHEST)


def on_device(
    leaf_area, soil_water, root_share, patch_weight, patch_owner, patch_local, month, mix
):
    months_count, types_here, cells_here = leaf_area.shape
    patch_count = patch_local.shape[0]
    owners = patch_owner[:, 0]
    cell_iota = jnp.arange(cells_here, dtype=jnp.int32)
    devices = lax.axis_size("blk")
    capacity = max(2, 2 * patch_count // devices)
    owner_table = (owners[:, None] == jnp.arange(devices, dtype=jnp.int32)[None, :]).astype(
        jnp.float32
    )
    patch_iota = jnp.arange(patch_count, dtype=jnp.int32)
    earlier = (patch_iota[:, None] > patch_iota[None, :]).astype(jnp.float32)
    before = exact_dot(earlier, owner_table)
    ranks = jnp.sum(before * owner_table, axis=1).astype(jnp.int32)
    slots = owners * capacity + ranks
    slot_iota = jnp.arange(devices * capacity, dtype=jnp.int32)
    slot_table = (slots[:, None] == slot_iota[None, :]).astype(jnp.float32)
    packed = jnp.concatenate([patch_weight, patch_local.astype(jnp.float32)[None, :]], axis=0)
    buffer = exact_dot(packed, slot_table)
    received = lax.all_to_all(buffer, "blk", split_axis=1, concat_axis=1, tiled=True)
    weights = received[:types_here]
    cell_ids = received[types_here].astype(jnp.int32)
    cell_table = (cell_iota[:, None] == cell_ids[None, :]).astype(jnp.float32)
    current = interpolate(leaf_area, month, mix)
    patch_leaf = exact_dot(current, cell_table)
    patch_soil = exact_dot(soil_water, cell_table)
    canopy = canopy_terms(weights, patch_leaf, patch_soil, root_share)
    grid_sum = exact_dot(canopy, cell_table.T)
    total = lax.psum(jnp.sum(grid_sum, axis=0), "layer")
    return grid_sum / (1.0 + total)


def solution(mesh):
    in_specs = (
        P(None, "layer", "blk"),
        P(None, "blk"),
        P("layer", None),
        P("layer", "blk"),
        P("blk", None),
        P("blk"),
        P(),
        P(),
    )
    out_specs = P("layer", "blk")
    return jax.shard_map(
        on_device, mesh=mesh, in_specs=in_specs, out_specs=out_specs, check_vma=False
    )
```

profile of v0, /device:TPU:0, one launch (start us, length us, event | category | flops | bytes accessed | tf_op | source)
XLA Modules:
  0.0 88.4 jit_solution(17370040293893275652)
XLA Ops:
  0.0 0.0 copy-start
  0.0 0.7 convert_element_type.30
  0.7 0.0 copy-start.2
  0.7 0.0 copy-start.1
  0.7 15.9 %fusion.13 = f32[4096]{0:T(1024)S(1)} fusion(s32[4096]{0:T(1024)} %bitcast.33), kind=kOutput, calls=%fused_computation.18 | convolution fusion | flops 285339648 | bytes 32768 | tf_op jit(solution)/shard_map/dot_general | solution.py:21
  16.7 0.0 copy-done.2
  16.7 0.0 copy-done.1
  16.7 43.1 %fusion = f32[5,8192]{1,0:T(8,128)} fusion(s32[4096]{0:T(1024)S(1)} %bitcast.34, f32[5,4096]{1,0:T(8,128)S(1)} %fusion.36), kind=kOutput, calls=%fused_computation.1 | convolution fusion | flops 2046820352 | bytes 262144 | tf_op jit(solution)/shard_map/dot_general | solution.py:21
  59.8 7.3 %all-to-all-start = ((f32[5,8,1024]{2,0,1:T(8,128)}), f32[5,8,1024]{2,0,1:T(8,128)S(1)}, u32[]{:S(2)}, u32[]{:S(2)}) async-start(f32[5,8,1024]{2,0,1:T(8,128)} %bitcast.4), calls=%async_computation | async-start | bytes 524288 | tf_op jit(solution)/shard_map/all_to_all | solution.py:45
  68.5 7.6 %all-to-all-done = f32[5,8,1024]{2,0,1:T(8,128)S(1)} async-done(((f32[5,8,1024]{2,0,1:T(8,128)}), f32[5,8,1024]{2,0,1:T(8,128)S(1)}, u32[]{:S(2)}, u32[]{:S(2)}) %all-to-all-start) | async-done | bytes 163872 | tf_op jit(solution)/shard_map/all_to_all | solution.py:45
  76.1 0.0 copy-done
  76.1 1.4 %fusion.9 = f32[8192,10]{0,1:T(8,128)S(1)} fusion(f32[10,128]{1,0:T(8,128)S(1)} %copy-done, s32[8192]{0:T(1024)S(1)} %bitcast.30), kind=kOutput, calls=%fused_computation.14 | convolution fusion | flops 126877696 | bytes 365568 | tf_op jit(solution)/shard_map/dot_general | solution.py:21
  77.6 0.0 copy-start.3
  77.6 2.1 %fusion.6 = f32[4,8192]{1,0:T(4,128)S(1)} fusion(f32[4,8192]{1,0:T(4,128)S(1)} %bitcast.27, s32[8192]{0:T(1024)S(1)} %bitcast.31, f32[12,4,128]{2,1,0:T(4,128)} %param.8, s32[]{:T(128)S(6)} %select_n.16, s32[]{:T(128)S(6)} %select_n.14, f32[]{:T(128)S(6)} %sub.10, f32[]{:T(128)} %bitcast.25), kind=kOutput, calls=%fused_computation.10 | convolution fusion | flops 51480064 | bytes 299532 | tf_op jit(solution)/shard_map/dot_general | solution.py:21
  79.7 0.0 copy-done.3
  79.7 0.4 fusion.3
  80.1 2.0 %fusion.28 = (f32[128]{0:T(128)S(1)}, f32[4,128]{1,0:T(4,128)S(1)}) fusion(f32[4,8192]{1,0:T(4,128)S(1)} %fusion.3, s32[8192]{0:T(1024)S(1)} %bitcast.32), kind=kOutput, calls=%fused_computation.38 | convolution fusion | flops 51380608 | bytes 166400 | tf_op jit(solution)/shard_map/dot_general | solution.py:21
  82.1 5.7 %psum.7 = f32[128]{0:T(128)S(1)} all-reduce(f32[128]{0:T(128)S(1)} %get-tuple-element.5), channel_id=1, replica_groups=mesh['blk'=8,'layer'=4] {'layer'}, use_global_device_ids=true, to_apply=%region_2.3 | all-reduce | flops 128 | bytes 1024 | tf_op jit(solution)/shard_map/psum | solution.py:54
  87.8 0.6 broadcast_divide_fusion
  (6 shorter events, 0.1 us)
Async XLA Ops:
  0.0 76.1 %copy-start = (f32[10,128]{1,0:T(8,128)S(1)}, f32[10,128]{1,0:T(8,128)}, u32[]{:S(2)}) copy-start(f32[10,128]{1,0:T(8,128)} %param.9) | copy-start | bytes 15364
  0.7 15.9 %copy-start.2 = (s32[4096,1]{0,1:T(1,128)S(1)}, s32[4096,1]{0,1:T(1,128)}, u32[]{:S(2)}) copy-start(s32[4096,1]{0,1:T(1,128)} %param.12) | copy-start | bytes 49156
  0.7 16.0 %copy-start.1 = (f32[4,4096]{1,0:T(4,128)S(1)}, f32[4,4096]{1,0:T(4,128)}, u32[]{:S(2)}) copy-start(f32[4,4096]{1,0:T(4,128)} %param.11) | copy-start | bytes 196612
  59.8 16.2 %all-to-all-start = ((f32[5,8,1024]{2,0,1:T(8,128)}), f32[5,8,1024]{2,0,1:T(8,128)S(1)}, u32[]{:S(2)}, u32[]{:S(2)}) async-start(f32[5,8,1024]{2,0,1:T(8,128)} %bitcast.4), calls=%async_computation | async-start | bytes 524288 | tf_op jit(solution)/shard_map/all_to_all | solution.py:45
  77.6 2.1 %copy-start.3 = (f32[4,10]{1,0:T(4,128)S(1)}, f32[4,10]{1,0:T(4,128)}, u32[]{:S(2)}) copy-start(f32[4,10]{1,0:T(4,128)} %param.10) | copy-start | bytes 484
where the time goes:
time: 88.8 us; the launch traced here: 88.4 us
  matrix products  64.9 us (73%)
  waiting for transfers between devices  7.59 us (9%)
  starting transfers between devices  7.31 us (8%)
  blocking collectives  5.67 us (6%)
  other arithmetic  1.43 us (2%)
  between operations  1.42 us (2%)
    dot_general x5, matrix products, exact_dot(): return jnp.dot(left, right, precision=lax.Precision.HIGHEST)  64.5 us
    all_to_all x1, waiting for transfers between devices, on_device(): lax.all_to_all(buffer, 'blk', split_axis=1, concat_axis=1, tiled=True)  7.59 us
    all_to_all x1, starting transfers between devices, on_device(): lax.all_to_all(buffer, 'blk', split_axis=1, concat_axis=1, tiled=True)  7.31 us
    psum x1, blocking collectives, on_device(): total = lax.psum(jnp.sum(grid_sum, axis=0), 'layer')  5.67 us
  transfers between devices with their start and end apart: 1, of which 1 were waited for; matrix products, arithmetic and copies ran while one was open for 0% of the time, Pallas kernels for 0%

commit v1 on v0

--- a/solution.py
+++ b/solution.py
@@ -42,7 +42,10 @@
     slot_table = (slots[:, None] == slot_iota[None, :]).astype(jnp.float32)
     packed = jnp.concatenate([patch_weight, patch_local.astype(jnp.float32)[None, :]], axis=0)
     buffer = exact_dot(packed, slot_table)
-    received = lax.all_to_all(buffer, "blk", split_axis=1, concat_axis=1, tiled=True)
+    peers = lax.axis_size("blk")
+    blocks = jnp.stack(jnp.split(buffer, peers, axis=1), axis=0)
+    blocks = lax.all_to_all(blocks, "blk", split_axis=0, concat_axis=0)
+    received = jnp.concatenate(blocks, axis=1)
     weights = received[:types_here]
     cell_ids = received[types_here].astype(jnp.int32)
     cell_table = (cell_iota[:, None] == cell_ids[None, :]).astype(jnp.float32)

time: 88.8 us -> 92.3 us (1.039)
  local copies, waits for them, and re-layouts: 0.04 us -> 4.89 us
    unnamed x8 -> x17, local copies, waits for them, and re-layouts: 0.02 us -> 4.25 us
where the time goes in v1:
time: 92.3 us; the launch traced here: 92 us
  matrix products  64.4 us (70%)
  waiting for transfers between devices  7.59 us (8%)
  starting transfers between devices  7.31 us (8%)
  blocking collectives  5.67 us (6%)
  local copies, waits for them, and re-layouts  4.89 us (5%)
  between operations  1.44 us (2%)
    dot_general x5, matrix products, exact_dot(): return jnp.dot(left, right, precision=lax.Precision.HIGHEST)  64 us
    all_to_all x1, waiting for transfers between devices, on_device(): blocks = lax.all_to_all(blocks, 'blk', split_axis=0, concat_axis=0)  7.59 us
    all_to_all x1, starting transfers between devices, on_device(): blocks = lax.all_to_all(blocks, 'blk', split_axis=0, concat_axis=0)  7.31 us
    psum x1, blocking collectives, on_device(): total = lax.psum(jnp.sum(grid_sum, axis=0), 'layer')  5.67 us
    unnamed x17, local copies, waits for them, and re-layouts  4.25 us
  transfers between devices with their start and end apart: 1, of which 1 were waited for; matrix products, arithmetic and copies ran while one was open for 0% of the time, Pallas kernels for 0%

profile of v1, /device:TPU:0, one launch (start us, length us, event | category | flops | bytes accessed | tf_op | source)
XLA Modules:
  0.0 92.0 jit_solution(532935269755276976)
XLA Ops:
  0.0 0.0 copy-start
  0.0 0.0 copy-start.2
  0.0 0.0 copy-start.3
  0.0 0.0 copy-start.1
  0.0 15.9 %fusion.13 = f32[4096]{0:T(1024)S(1)} fusion(s32[4096]{0:T(1024)} %bitcast.67), kind=kOutput, calls=%fused_computation.18 | convolution fusion | flops 285339648 | bytes 32768 | tf_op jit(solution)/shard_map/dot_general | solution.py:21
  16.0 0.0 copy-done.2
  16.0 0.0 copy-done.3
  16.0 0.0 copy-done.1
  16.1 42.5 %fusion = f32[5,8192]{1,0:T(8,128)S(1)} fusion(s32[4096]{0:T(1024)S(1)} %bitcast.68, f32[5,4096]{1,0:T(8,128)S(1)} %fusion.44), kind=kOutput, calls=%fused_computation.1 | convolution fusion | flops 2046820352 | bytes 262144 | tf_op jit(solution)/shard_map/dot_general | solution.py:21
  58.6 0.6 fusion.25
  59.2 0.6 fusion.24
  59.8 0.6 fusion.23
  60.4 0.6 fusion.22
  61.0 0.6 fusion.21
  61.6 0.6 fusion.20
  62.2 0.6 fusion.19
  62.8 0.6 fusion.18
  63.4 7.3 %all-to-all-start = ((f32[8,5,1024]{2,1,0:T(8,128)}), f32[8,5,1024]{2,1,0:T(8,128)S(1)}, u32[]{:S(2)}, u32[]{:S(2)}) async-start(f32[8,5,1024]{2,1,0:T(8,128)} %fusion.18), calls=%async_computation | async-start | bytes 524288 | tf_op jit(solution)/shard_map/all_to_all | solution.py:47
  72.1 7.6 %all-to-all-done = f32[8,5,1024]{2,1,0:T(8,128)S(1)} async-done(((f32[8,5,1024]{2,1,0:T(8,128)}), f32[8,5,1024]{2,1,0:T(8,128)S(1)}, u32[]{:S(2)}, u32[]{:S(2)}) %all-to-all-start) | async-done | bytes 163872 | tf_op jit(solution)/shard_map/all_to_all | solution.py:47
  79.8 0.0 copy-done
  79.8 1.4 %fusion.9 = f32[8192,10]{0,1:T(8,128)S(1)} fusion(f32[10,128]{1,0:T(8,128)S(1)} %copy-done, s32[8192]{0:T(1024)S(1)} %bitcast.64), kind=kOutput, calls=%fused_computation.14 | convolution fusion | flops 126877696 | bytes 365568 | tf_op jit(solution)/shard_map/dot_general | solution.py:21
  81.2 0.0 copy-start.4
  81.2 2.1 %fusion.6 = f32[4,8192]{1,0:T(4,128)S(1)} fusion(f32[4,8192]{1,0:T(4,128)S(1)} %bitcast.61, s32[8192]{0:T(1024)S(1)} %bitcast.65, f32[12,4,128]{2,1,0:T(4,128)} %param.8, s32[]{:T(128)S(6)} %select_n.16, s32[]{:T(128)S(6)} %select_n.14, f32[]{:T(128)S(6)} %sub.10, f32[]{:T(128)} %bitcast.57), kind=kOutput, calls=%fused_computation.10 | convolution fusion | flops 51480064 | bytes 299532 | tf_op jit(solution)/shard_map/dot_general | solution.py:21
  83.3 0.0 copy-done.4
  83.3 0.4 fusion.3
  83.7 2.0 %fusion.36 = (f32[128]{0:T(128)S(1)}, f32[4,128]{1,0:T(4,128)S(1)}) fusion(f32[4,8192]{1,0:T(4,128)S(1)} %fusion.3, s32[8192]{0:T(1024)S(1)} %bitcast.66), kind=kOutput, calls=%fused_computation.54 | convolution fusion | flops 51380608 | bytes 166400 | tf_op jit(solution)/shard_map/dot_general | solution.py:21
  85.7 5.7 %psum.7 = f32[128]{0:T(128)S(1)} all-reduce(f32[128]{0:T(128)S(1)} %get-tuple-element.5), channel_id=1, replica_groups=mesh['blk'=8,'layer'=4] {'layer'}, use_global_device_ids=true, to_apply=%region_2.3 | all-reduce | flops 128 | bytes 1024 | tf_op jit(solution)/shard_map/psum | solution.py:57
  91.4 0.6 broadcast_divide_fusion
  (7 shorter events, 0.1 us)
Async XLA Ops:
  0.0 79.8 %copy-start = (f32[10,128]{1,0:T(8,128)S(1)}, f32[10,128]{1,0:T(8,128)}, u32[]{:S(2)}) copy-start(f32[10,128]{1,0:T(8,128)} %param.9) | copy-start | bytes 15364
  0.0 16.0 %copy-start.2 = (s32[4096,1]{0,1:T(1,128)S(1)}, s32[4096,1]{0,1:T(1,128)}, u32[]{:S(2)}) copy-start(s32[4096,1]{0,1:T(1,128)} %param.12) | copy-start | bytes 49156
  0.0 16.0 %copy-start.3 = (s32[4096]{0:T(1024)S(1)}, s32[4096]{0:T(1024)}, u32[]{:S(2)}) copy-start(s32[4096]{0:T(1024)} %param.13) | copy-start | bytes 49156
  0.0 16.0 %copy-start.1 = (f32[4,4096]{1,0:T(4,128)S(1)}, f32[4,4096]{1,0:T(4,128)}, u32[]{:S(2)}) copy-start(f32[4,4096]{1,0:T(4,128)} %param.11) | copy-start | bytes 196612
  63.4 16.2 %all-to-all-start = ((f32[8,5,1024]{2,1,0:T(8,128)}), f32[8,5,1024]{2,1,0:T(8,128)S(1)}, u32[]{:S(2)}, u32[]{:S(2)}) async-start(f32[8,5,1024]{2,1,0:T(8,128)} %fusion.18), calls=%async_computation | async-start | bytes 524288 | tf_op jit(solution)/shard_map/all_to_all | solution.py:47
  81.2 2.1 %copy-start.4 = (f32[4,10]{1,0:T(4,128)S(1)}, f32[4,10]{1,0:T(4,128)}, u32[]{:S(2)}) copy-start(f32[4,10]{1,0:T(4,128)} %param.10) | copy-start | bytes 484

commit v2 on v0

--- a/solution.py
+++ b/solution.py
@@ -51,7 +51,11 @@
     patch_soil = exact_dot(soil_water, cell_table)
     canopy = canopy_terms(weights, patch_leaf, patch_soil, root_share)
     grid_sum = exact_dot(canopy, cell_table.T)
-    total = lax.psum(jnp.sum(grid_sum, axis=0), "layer")
+
+    def _cover_results(values, peer_axis):
+        return jnp.sum(lax.all_gather(values, peer_axis), 0)
+
+    total = _cover_results(jnp.sum(grid_sum, axis=0), "layer")
     return grid_sum / (1.0 + total)
 
 

time: 88.8 us -> 88.2 us (level)
    psum x1 -> x0, blocking collectives: 5.67 us -> none  [on_device(): total = lax.psum(jnp.sum(grid_sum, axis=0), 'layer')]
    all_gather x0 -> x1, blocking collectives: none -> 5.06 us  [_cover_results(): return jnp.sum(lax.all_gather(values, peer_axis), 0)]
where the time goes in v2:
time: 88.2 us; the launch traced here: 87.8 us
  matrix products  64.9 us (74%)
  waiting for transfers between devices  7.59 us (9%)
  starting transfers between devices  7.31 us (8%)
  blocking collectives  5.06 us (6%)
  other arithmetic  1.45 us (2%)
  between operations  1.42 us (2%)
    dot_general x5, matrix products, exact_dot(): return jnp.dot(left, right, precision=lax.Precision.HIGHEST)  64.5 us
    all_to_all x1, waiting for transfers between devices, on_device(): lax.all_to_all(buffer, 'blk', split_axis=1, concat_axis=1, tiled=True)  7.59 us
    all_to_all x1, starting transfers between devices, on_device(): lax.all_to_all(buffer, 'blk', split_axis=1, concat_axis=1, tiled=True)  7.31 us
    all_gather x1, blocking collectives, _cover_results(): return jnp.sum(lax.all_gather(values, peer_axis), 0)  5.06 us
  transfers between devices with their start and end apart: 1, of which 1 were waited for; matrix products, arithmetic and copies ran while one was open for 0% of the time, Pallas kernels for 0%

profile of v2, /device:TPU:0, one launch (start us, length us, event | category | flops | bytes accessed | tf_op | source)
XLA Modules:
  0.0 87.8 jit_solution(15992603263277448623)
XLA Ops:
  0.0 0.0 copy-start
  0.0 0.7 convert_element_type.30
  0.7 0.0 copy-start.2
  0.7 0.0 copy-start.1
  0.7 15.9 %fusion.13 = f32[4096]{0:T(1024)S(1)} fusion(s32[4096]{0:T(1024)} %bitcast.34), kind=kOutput, calls=%fused_computation.18 | convolution fusion | flops 285339648 | bytes 32768 | tf_op jit(solution)/shard_map/dot_general | solution.py:21
  16.7 0.0 copy-done.2
  16.7 0.0 copy-done.1
  16.7 43.1 %fusion = f32[5,8192]{1,0:T(8,128)} fusion(s32[4096]{0:T(1024)S(1)} %bitcast.35, f32[5,4096]{1,0:T(8,128)S(1)} %fusion.36), kind=kOutput, calls=%fused_computation.1 | convolution fusion | flops 2046820352 | bytes 262144 | tf_op jit(solution)/shard_map/dot_general | solution.py:21
  59.8 7.3 %all-to-all-start = ((f32[5,8,1024]{2,0,1:T(8,128)}), f32[5,8,1024]{2,0,1:T(8,128)S(1)}, u32[]{:S(2)}, u32[]{:S(2)}) async-start(f32[5,8,1024]{2,0,1:T(8,128)} %bitcast.4), calls=%async_computation | async-start | bytes 524288 | tf_op jit(solution)/shard_map/all_to_all | solution.py:45
  68.5 7.6 %all-to-all-done = f32[5,8,1024]{2,0,1:T(8,128)S(1)} async-done(((f32[5,8,1024]{2,0,1:T(8,128)}), f32[5,8,1024]{2,0,1:T(8,128)S(1)}, u32[]{:S(2)}, u32[]{:S(2)}) %all-to-all-start) | async-done | bytes 163872 | tf_op jit(solution)/shard_map/all_to_all | solution.py:45
  76.1 0.0 copy-done
  76.1 1.4 %fusion.9 = f32[8192,10]{0,1:T(8,128)S(1)} fusion(f32[10,128]{1,0:T(8,128)S(1)} %copy-done, s32[8192]{0:T(1024)S(1)} %bitcast.31), kind=kOutput, calls=%fused_computation.14 | convolution fusion | flops 126877696 | bytes 365568 | tf_op jit(solution)/shard_map/dot_general | solution.py:21
  77.6 0.0 copy-start.3
  77.6 2.1 %fusion.6 = f32[4,8192]{1,0:T(4,128)S(1)} fusion(f32[4,8192]{1,0:T(4,128)S(1)} %bitcast.28, s32[8192]{0:T(1024)S(1)} %bitcast.32, f32[12,4,128]{2,1,0:T(4,128)} %param.8, s32[]{:T(128)S(6)} %select_n.16, s32[]{:T(128)S(6)} %select_n.14, f32[]{:T(128)S(6)} %sub.10, f32[]{:T(128)} %bitcast.26), kind=kOutput, calls=%fused_computation.10 | convolution fusion | flops 51480064 | bytes 299532 | tf_op jit(solution)/shard_map/dot_general | solution.py:21
  79.7 0.0 copy-done.3
  79.7 0.4 fusion.3
  80.1 2.0 %fusion.28 = (f32[128]{0:T(128)S(1)}, f32[4,128]{1,0:T(4,128)S(1)}) fusion(f32[4,8192]{1,0:T(4,128)S(1)} %fusion.3, s32[8192]{0:T(1024)S(1)} %bitcast.33), kind=kOutput, calls=%fused_computation.38 | convolution fusion | flops 51380608 | bytes 166400 | tf_op jit(solution)/shard_map/dot_general | solution.py:21
  82.1 5.1 %all-gather.1 = f32[4,1,128]{2,1,0:T(1,128)S(1)} all-gather(f32[1,1,128]{2,1,0:T(1,128)S(1)} %bitcast.36), channel_id=2, replica_groups=mesh['blk'=8,'layer'=4] {'layer'}, dimensions={0}, use_global_device_ids=true | all-gather | bytes 2560 | tf_op jit(solution)/shard_map/all_gather | solution.py:56
  87.2 0.6 broadcast_divide_fusion
  (7 shorter events, 0.2 us)
Async XLA Ops:
  0.0 76.1 %copy-start = (f32[10,128]{1,0:T(8,128)S(1)}, f32[10,128]{1,0:T(8,128)}, u32[]{:S(2)}) copy-start(f32[10,128]{1,0:T(8,128)} %param.9) | copy-start | bytes 15364
  0.7 15.9 %copy-start.2 = (s32[4096,1]{0,1:T(1,128)S(1)}, s32[4096,1]{0,1:T(1,128)}, u32[]{:S(2)}) copy-start(s32[4096,1]{0,1:T(1,128)} %param.12) | copy-start | bytes 49156
  0.7 16.0 %copy-start.1 = (f32[4,4096]{1,0:T(4,128)S(1)}, f32[4,4096]{1,0:T(4,128)}, u32[]{:S(2)}) copy-start(f32[4,4096]{1,0:T(4,128)} %param.11) | copy-start | bytes 196612
  59.8 16.2 %all-to-all-start = ((f32[5,8,1024]{2,0,1:T(8,128)}), f32[5,8,1024]{2,0,1:T(8,128)S(1)}, u32[]{:S(2)}, u32[]{:S(2)}) async-start(f32[5,8,1024]{2,0,1:T(8,128)} %bitcast.4), calls=%async_computation | async-start | bytes 524288 | tf_op jit(solution)/shard_map/all_to_all | solution.py:45
  77.6 2.1 %copy-start.3 = (f32[4,10]{1,0:T(4,128)S(1)}, f32[4,10]{1,0:T(4,128)}, u32[]{:S(2)}) copy-start(f32[4,10]{1,0:T(4,128)} %param.10) | copy-start | bytes 484
